TPU v7x, 32 devices: a whole 2x2x4 slice. The times are simulated.
32 devices in a mesh: role: 4 (over z), dp: 2 (over x), tp: 4 (over y, core).
Axes of the slice: x: 2, y: 2, z: 4, core: 2. Of those that a mesh axis runs over, the one named last changes fastest.
Arguments:
- activations: bfloat16 [2048, 8192], P(('role', 'dp'), 'tp'), may hold values from -6 to 6
- cotangent: bfloat16 [2048, 14336], P(('role', 'dp'), 'tp'), may hold values from -6 to 6
- block_keep: int32 [8], P(('role', 'dp')), may hold values 0 or 1
- input_factor: float32 [64, 8192], P(('role', 'dp'), 'tp'), may hold values from -0.5 to 0.5
- input_mean: float32 [64, 8192], P(('role', 'dp'), 'tp'), may hold values from -6 to 6
- input_square: float32 [64, 8192], P(('role', 'dp'), 'tp'), may hold values from 0.5 to 4
- output_factor: float32 [64, 14336], P(('role', 'dp'), 'tp'), may hold values from -0.3125 to 0.3125
- output_mean: float32 [64, 14336], P(('role', 'dp'), 'tp'), may hold values from -6 to 6
- output_square: float32 [64, 14336], P(('role', 'dp'), 'tp'), may hold values from 0.5 to 4
- frozen_base_rows: bfloat16 [14336, 8192], P(('dp', 'tp')), may hold values from -0.0625 to 0.0625
- prompts: bfloat16 [1024, 8192], P(('role', 'dp', 'tp')), may hold values from -6 to 6
Outputs:
- updated_input: float32 [64, 8192], P(('role', 'dp'), 'tp')
- updated_output: float32 [64, 14336], P(('role', 'dp'), 'tp')
- mean_input: float32 [64, 8192], P(('role', 'dp'), 'tp')
- mean_output: float32 [64, 14336], P(('role', 'dp'), 'tp')
- square_input: float32 [64, 8192], P(('role', 'dp'), 'tp')
- square_output: float32 [64, 14336], P(('role', 'dp'), 'tp')
- merged_weight_rows: bfloat16 [14336, 8192], P(('dp', 'tp'))
- projected: bfloat16 [14336, 1024], P(('dp', 'tp'), 'role')
All inputs are finite; a program needn't handle non-finite values. No bound on the sum of `block_keep` on one device may be relied on, other than what follows from the above.
Results may differ from a plain program's by a relative error of at most 0.006.
Values may be sent and summed in bfloat16 or wider, within the bound.
A program may use at most 128 MiB of HBM per device.

v0:
```python
import jax
import jax.numpy as jnp
from jax import lax
from jax.sharding import PartitionSpec as P

ROLLOUT_TOKENS = 256
adapter_scale = 2.0
learn_rate = 0.004
beta_one = 0.9
beta_two = 0.95
epsilon = 1e-08
first_fix = 1.0 - 0.9**20
second_fix = 1.0 - 0.95**20


def adam_update(factor, moment, square, gradient):
    moment_new = beta_one * moment + (1.0 - beta_one) * gradient
    square_new = beta_two * square + (1.0 - beta_two) * gradient * gradient
    factor_new = factor - learn_rate * (moment_new / first_fix) / (
        jnp.sqrt(square_new / second_fix) + epsilon
    )
    return (factor_new, moment_new, square_new)


def masked(values, block_keep):
    blocks = block_keep.shape[0]
    reshaped_rows = values.reshape(blocks, values.shape[0] // blocks, values.shape[1])
    weighted = reshaped_rows * block_keep.astype(jnp.float32)[:, None, None]
    return weighted.reshape(values.shape).astype(jnp.bfloat16)


def contract_rows(left, right):
    return lax.dot_general(
        left, right, (((0,), (0,)), ((), ())), preferred_element_type=jnp.float32
    )


def contract_cols(left, right):
    return lax.dot_general(
        left, right, (((1,), (1,)), ((), ())), preferred_element_type=jnp.float32
    )


def body(
    activations,
    cotangent,
    block_keep,
    input_factor,
    input_mean,
    input_square,
    output_factor,
    output_mean,
    output_square,
    frozen_base_rows,
    prompts,
):
    input_rows, output_rows = (
        lax.all_gather(input_factor.astype(jnp.bfloat16), ("role", "dp"), axis=0, tiled=True),
        lax.all_gather(output_factor.astype(jnp.bfloat16), ("role", "dp"), axis=0, tiled=True),
    )
    low_input = jnp.dot(activations, input_rows.T, preferred_element_type=jnp.float32)
    low_grad = jnp.dot(cotangent, output_rows.T, preferred_element_type=jnp.float32)
    low_input, low_grad = lax.psum((low_input, low_grad), "tp")
    input_kept = masked(low_input, block_keep)
    grad_kept = masked(low_grad, block_keep)
    input_part = contract_rows(grad_kept, activations)
    output_part = contract_rows(input_kept, cotangent)
    group_input, group_output = (
        lax.psum_scatter(input_part, "role", scatter_dimension=0, tiled=True),
        lax.psum_scatter(output_part, "role", scatter_dimension=0, tiled=True),
    )
    input_sum, output_sum = (
        lax.psum_scatter(group_input, "dp", scatter_dimension=0, tiled=True),
        lax.psum_scatter(group_output, "dp", scatter_dimension=0, tiled=True),
    )
    adapter_factor_scale = adapter_scale / ROLLOUT_TOKENS
    input_new, input_moment, input_second = adam_update(
        input_factor, input_mean, input_square, input_sum * adapter_factor_scale
    )
    output_new, output_moment, output_second = adam_update(
        output_factor, output_mean, output_square, output_sum * adapter_factor_scale
    )
    input_send = input_new.astype(jnp.bfloat16)
    output_send = output_new.astype(jnp.bfloat16)
    input_cols, output_cols = (
        lax.all_gather(input_send, ("role", "dp"), axis=0, tiled=True),
        lax.all_gather(output_send, ("role", "dp"), axis=0, tiled=True),
    )
    input_whole, output_whole = (
        lax.all_gather(input_cols, "tp", axis=1, tiled=True),
        lax.all_gather(output_cols, "tp", axis=1, tiled=True),
    )
    rows_here = frozen_base_rows.shape[0]
    row_block = lax.axis_index("dp") * lax.axis_size("tp") + lax.axis_index("tp")
    output_slice = lax.dynamic_slice_in_dim(output_whole, row_block * rows_here, rows_here, 1)
    adapter_delta_rows = contract_rows(output_slice, input_whole)
    merged_weight_rows = (
        frozen_base_rows.astype(jnp.float32) + adapter_scale * adapter_delta_rows
    ).astype(jnp.bfloat16)
    group_prompts = lax.all_gather(prompts, ("dp", "tp"), axis=0, tiled=True)
    projected = contract_cols(merged_weight_rows, group_prompts)
    return (
        input_new,
        output_new,
        input_moment,
        output_moment,
        input_second,
        output_second,
        merged_weight_rows,
        projected.astype(jnp.bfloat16),
    )


def solution(mesh):
    placed = (
        P(("role", "dp"), "tp"),
        P(("role", "dp"), "tp"),
        P(("role", "dp")),
        P(("role", "dp"), "tp"),
        P(("role", "dp"), "tp"),
        P(("role", "dp"), "tp"),
        P(("role", "dp"), "tp"),
        P(("role", "dp"), "tp"),
        P(("role", "dp"), "tp"),
        P(("dp", "tp"), None),
        P(("role", "dp", "tp"), None),
    )
    return jax.shard_map(
        body,
        mesh=mesh,
        in_specs=placed,
        out_specs=(
            P(("role", "dp"), "tp"),
            P(("role", "dp"), "tp"),
            P(("role", "dp"), "tp"),
            P(("role", "dp"), "tp"),
            P(("role", "dp"), "tp"),
            P(("role", "dp"), "tp"),
            P(("dp", "tp"), None),
            P(("dp", "tp"), "role"),
        ),
        check_vma=False,
    )
```

profile of v0, /device:TPU:0, one launch (start us, length us, event | category | flops | bytes accessed | tf_op | source)
XLA Modules:
  0.0 323.7 jit_solution(6785489352362475291)
XLA Ops:
  7.2 1.1 convert_element_type.31
  8.3 32.9 %all_gather.21 = bf16[64,3584]{1,0:T(8,128)(2,1)S(1)} all-gather(bf16[8,3584]{1,0:T(8,128)(2,1)S(1)} %convert_element_type.31), channel_id=1, replica_groups=mesh['role'=4,'dp'=2,'tp'=4] {'role','dp'}, dimensions={0}, use_global_device_ids=true | all-gather | bytes 516096 | tf_op jit(solution)/shard_map/all_gather | solution.py:59
  41.2 0.8 convert_element_type.34
  42.0 30.7 %all_gather.22 = bf16[64,2048]{1,0:T(8,128)(2,1)S(1)} all-gather(bf16[8,2048]{1,0:T(8,128)(2,1)S(1)} %convert_element_type.34), channel_id=1, replica_groups=mesh['role'=4,'dp'=2,'tp'=4] {'role','dp'}, dimensions={0}, use_global_device_ids=true | all-gather | bytes 294912 | tf_op jit(solution)/shard_map/all_gather | solution.py:58
  72.7 1.3 fusion.8
  74.0 2.3 fusion.9
  77.2 32.8 %all-reduce.3.cloned.1.call-done = (f32[256,64]{1,0:T(8,128)}, f32[256,64]{1,0:T(8,128)}) async-done(((f32[256,64]{1,0:T(8,128)}, f32[256,64]{1,0:T(8,128)}), (f32[256,64]{1,0:T(8,128)}, f32[256,64]{1,0:T(8,128)})) %all-reduce.3.cloned.1.call-update) | async-done | bytes 131088 | tf_op jit(solution)/shard_map/psum | solution.py:63
  110.0 2.0 fusion.1
  112.0 0.0 reduce-scatter.9.cloned.1.call-start
  112.1 2.3 fusion.2
  114.4 20.2 %reduce-scatter.5.cloned.1.call-done = f32[16,2048]{1,0:T(8,128)} async-done(((f32[64,2048]{1,0:T(8,128)}), f32[16,2048]{1,0:T(8,128)}) %reduce-scatter.5.cloned.1.call-update) | async-done | bytes 131088 | tf_op jit(solution)/shard_map/reduce_scatter | solution.py:69
  134.7 26.3 %reduce-scatter.9.cloned.1.call-done = f32[16,3584]{1,0:T(8,128)} async-done(((f32[64,3584]{1,0:T(8,128)}), f32[16,3584]{1,0:T(8,128)}) %reduce-scatter.9.cloned.1.call-update) | async-done | bytes 229392 | tf_op jit(solution)/shard_map/reduce_scatter | solution.py:70
  161.1 11.3 %reduce-scatter.7.cloned.1.call-done = f32[8,2048]{1,0:T(8,128)} async-done(((f32[16,2048]{1,0:T(8,128)}), f32[8,2048]{1,0:T(8,128)}) %reduce-scatter.7.cloned.1.call-update) | async-done | bytes 65552 | tf_op jit(solution)/shard_map/reduce_scatter | solution.py:73
  172.4 1.5 fusion.7
  173.9 32.9 %all_gather.25 = bf16[64,2048]{1,0:T(8,128)(2,1)} all-gather(bf16[8,2048]{1,0:T(8,128)(2,1)S(1)} %get-tuple-element.14), channel_id=1, replica_groups=mesh['role'=4,'dp'=2,'tp'=4] {'role','dp'}, dimensions={0}, use_global_device_ids=true | all-gather | bytes 294912 | tf_op jit(solution)/shard_map/all_gather | solution.py:86
  206.8 0.0 all-gather.4.cloned.1.call-start
  206.9 1.7 fusion.6
  208.6 33.1 %all_gather.23 = bf16[64,3584]{1,0:T(8,128)(2,1)} all-gather(bf16[8,3584]{1,0:T(8,128)(2,1)S(1)} %get-tuple-element.10), channel_id=1, replica_groups=mesh['role'=4,'dp'=2,'tp'=4] {'role','dp'}, dimensions={0}, use_global_device_ids=true | all-gather | bytes 516096 | tf_op jit(solution)/shard_map/all_gather | solution.py:87
  241.7 0.0 all-gather.8.cloned.1.call-start
  241.7 0.7 all-gather.8.cloned.1.call-update
  242.5 20.4 %all-gather.4.cloned.1.call-done = bf16[64,14336]{1,0:T(8,128)(2,1)} async-done(((bf16[64,3584]{1,0:T(8,128)(2,1)}), bf16[64,14336]{1,0:T(8,128)(2,1)}) %all-gather.4.cloned.1.call-update) | async-done | bytes 1835024 | tf_op jit(solution)/shard_map/all_gather | solution.py:91
  262.9 23.8 %add_convert_fusion = bf16[1792,8192]{1,0:T(8,128)(2,1)} fusion(bf16[1792,8192]{1,0:T(8,128)(2,1)} %param.20, bf16[64,8192]{1,0:T(8,128)(2,1)} %all-gather.6.cloned.1.call-done, bf16[64,14336]{1,0:T(8,128)(2,1)} %all-gather.4.cloned.1.call-done, s32[]{:T(128)S(6)} %select_n.3), kind=kOutput, calls=%fused_computation | convolution fusion | flops 1937768448 | bytes 59998212 | tf_op jit(solution)/shard_map/dot_general | solution.py:33
  286.7 14.7 %all-gather.8.cloned.1.call-done = bf16[256,8192]{1,0:T(8,128)(2,1)} async-done(((bf16[32,8192]{1,0:T(8,128)(2,1)}), bf16[256,8192]{1,0:T(8,128)(2,1)}) %all-gather.8.cloned.1.call-update) | async-done | bytes 4194320 | tf_op jit(solution)/shard_map/all_gather | solution.py:100
  301.4 15.4 %convolution_convert_fusion = bf16[1792,256]{1,0:T(8,128)(2,1)} fusion(bf16[1792,8192]{1,0:T(8,128)(2,1)} %add_convert_fusion, bf16[256,8192]{1,0:T(8,128)(2,1)} %all-gather.8.cloned.1.call-done), kind=kOutput, calls=%fused_computation.1 | convolution fusion | flops 7516651520 | bytes 34471936 | tf_op jit(solution)/shard_map/dot_general | solution.py:39
  (32 shorter events, 0.4 us)
Async XLA Ops:
  7.2 65.6 %copy-start = (bf16[256,3584]{1,0:T(8,128)(2,1)S(1)}, bf16[256,3584]{1,0:T(8,128)(2,1)}, u32[]{:S(2)}) copy-start(bf16[256,3584]{1,0:T(8,128)(2,1)} %param.12) | copy-start | bytes 5505028
  7.2 102.8 %copy-start.2 = (bf16[256,2048]{1,0:T(8,128)(2,1)S(1)}, bf16[256,2048]{1,0:T(8,128)(2,1)}, u32[]{:S(2)}) copy-start(bf16[256,2048]{1,0:T(8,128)(2,1)} %param.11) | copy-start | bytes 3145732
  7.2 102.8 %all-reduce.3.cloned.1.call-start = ((), (), s32[]{:S(2)}) async-start(), calls=%async_computation.11 | async-start | bytes 524288 | tf_op jit(solution)/shard_map/psum | solution.py:63
  74.0 98.4 %copy-start.4 = (f32[8,2048]{1,0:T(8,128)S(1)}, f32[8,2048]{1,0:T(8,128)}, u32[]{:S(2)}) copy-start(f32[8,2048]{1,0:T(8,128)} %param.14) | copy-start | bytes 196612
  74.0 98.4 %copy-start.7 = (f32[8,2048]{1,0:T(8,128)S(1)}, f32[8,2048]{1,0:T(8,128)}, u32[]{:S(2)}) copy-start(f32[8,2048]{1,0:T(8,128)} %param.15) | copy-start | bytes 196612
  74.0 98.4 %copy-start.8 = (f32[8,2048]{1,0:T(8,128)S(1)}, f32[8,2048]{1,0:T(8,128)}, u32[]{:S(2)}) copy-start(f32[8,2048]{1,0:T(8,128)} %param.16) | copy-start | bytes 196612
  76.4 130.6 %copy-start.3 = (f32[8,3584]{1,0:T(8,128)S(1)}, f32[8,3584]{1,0:T(8,128)}, u32[]{:S(2)}) copy-start(f32[8,3584]{1,0:T(8,128)} %param.17) | copy-start | bytes 344068
  76.4 130.6 %copy-start.5 = (f32[8,3584]{1,0:T(8,128)S(1)}, f32[8,3584]{1,0:T(8,128)}, u32[]{:S(2)}) copy-start(f32[8,3584]{1,0:T(8,128)} %param.18) | copy-start | bytes 344068
  76.4 130.6 %copy-start.6 = (f32[8,3584]{1,0:T(8,128)S(1)}, f32[8,3584]{1,0:T(8,128)}, u32[]{:S(2)}) copy-start(f32[8,3584]{1,0:T(8,128)} %param.19) | copy-start | bytes 344068
  76.4 58.3 %reduce-scatter.5.cloned.1.call-start = ((), (), s32[]{:S(2)}) async-start(), calls=%async_computation.4 | async-start | bytes 655360 | tf_op jit(solution)/shard_map/reduce_scatter | solution.py:69
  112.0 49.0 %reduce-scatter.9.cloned.1.call-start = ((), (), s32[]{:S(2)}) async-start(), calls=%async_computation.6 | async-start | bytes 1146880 | tf_op jit(solution)/shard_map/reduce_scatter | solution.py:70
  114.4 58.0 %reduce-scatter.7.cloned.1.call-start = ((), (), s32[]{:S(2)}) async-start(), calls=%async_computation.5 | async-start | bytes 196608 | tf_op jit(solution)/shard_map/reduce_scatter | solution.py:73
  134.7 72.2 %reduce-scatter.11.cloned.1.call-start = ((), (), s32[]{:S(2)}) async-start(), calls=%async_computation.7 | async-start | bytes 344064 | tf_op jit(solution)/shard_map/reduce_scatter | solution.py:74
  161.1 81.4 %all-gather.6.cloned.1.call-start = ((), (), s32[]{:S(2)}) async-start(), calls=%async_computation.9 | async-start | bytes 1310720 | tf_op jit(solution)/shard_map/all_gather | solution.py:90
  206.8 56.1 %all-gather.4.cloned.1.call-start = ((), (), s32[]{:S(2)}) async-start(), calls=%async_computation.8 | async-start | bytes 2293760 | tf_op jit(solution)/shard_map/all_gather | solution.py:91
  241.7 59.7 %all-gather.8.cloned.1.call-start = ((), (), s32[]{:S(2)}) async-start(), calls=%async_computation.10 | async-start | bytes 4718592 | tf_op jit(solution)/shard_map/all_gather | solution.py:100
  301.4 15.4 %copy-start.1 = (bf16[256,3584]{1,0:T(8,128)(2,1)S(1)}, bf16[256,3584]{1,0:T(8,128)(2,1)}, u32[]{:S(2)}) copy-start(bf16[256,3584]{1,0:T(8,128)(2,1)} %param.12) | copy-start | bytes 5505028
Sparse Core Ops, SparseCore 0:
  76.5 33.4 all-reduce.2
  112.8 21.8 reduce-scatter.4
  137.6 23.4 reduce-scatter.8
  163.1 9.2 reduce-scatter.6
  174.5 11.9 reduce-scatter.10
  207.0 16.5 all-gather.5
  241.8 21.0 all-gather.3
  264.8 36.5 all-gather.7
where the time goes:
time: 324 us
  blocking collectives  130 us (40%)
  waiting for transfers between devices  127 us (39%)
  matrix products  47.2 us (15%)
  between operations  14.9 us (5%)
  other arithmetic  5.1 us (2%)
    all_gather x1, blocking collectives, body(): lax.all_gather(output_send, ('role', 'dp'), axis=0, tiled=True)  33.1 us
    all_gather x1, blocking collectives, body(): lax.all_gather(input_send, ('role', 'dp'), axis=0, tiled=True)  32.9 us
    all_gather x1, blocking collectives, body(): lax.all_gather(output_factor.astype(jnp.bfloat16), ('role', 'dp'), axis=0...  32.9 us
    psum x1, waiting for transfers between devices, body(): low_input, low_grad = lax.psum((low_input, low_grad), 'tp')  32.8 us
    all_gather x1, blocking collectives, body(): lax.all_gather(input_factor.astype(jnp.bfloat16), ('role', 'dp'), axis=0,...  30.7 us
    dot_general x3, matrix products, contract_rows(): lax.dot_general(left, right, (((0,), (0,)), ((), ())), preferred_element_...  28.1 us
    reduce_scatter x1, waiting for transfers between devices, body(): lax.psum_scatter(output_part, 'role', scatter_dimension=0, tiled=True)  26.3 us
    all_gather x1, waiting for transfers between devices, body(): lax.all_gather(output_cols, 'tp', axis=1, tiled=True)  20.4 us
  transfers between devices with their start and end apart: 8, of which 6 were waited for; matrix products, arithmetic and copies ran while one was open for 9% of the time, Pallas kernels for 0%

commit v1 on v0

--- a/solution.py
+++ b/solution.py
@@ -88,7 +88,7 @@
     )
     input_whole, output_whole = (
         lax.all_gather(input_cols, "tp", axis=1, tiled=True),
-        lax.all_gather(output_cols, "tp", axis=1, tiled=True),
+        jnp.concatenate(lax.all_gather(output_cols, "tp"), axis=1),
     )
     rows_here = frozen_base_rows.shape[0]
     row_block = lax.axis_index("dp") * lax.axis_size("tp") + lax.axis_index("tp")

time: 324 us -> 321 us (level)
  waiting for transfers between devices: 127 us -> 119 us
  local copies, waits for them, and re-layouts: 0.04 us -> 4.53 us
    all_gather x1, waiting for transfers between devices: 20.4 us -> 0.02 us  [body(): lax.all_gather(output_cols, 'tp')]
    reduce_scatter x1, waiting for transfers between devices: 0.02 us -> 11.7 us  [body(): lax.psum_scatter(group_output, 'dp', scatter_dimension=0, tiled=True)]
    all_gather x1, waiting for transfers between devices: 0.02 us -> 11.4 us  [body(): lax.all_gather(input_cols, 'tp', axis=1, tiled=True)]
    reduce_scatter x1, waiting for transfers between devices: 11.3 us -> 0.02 us  [body(): lax.psum_scatter(group_input, 'dp', scatter_dimension=0, tiled=True)]
    reduce_scatter x1, waiting for transfers between devices: 20.2 us -> 23.5 us  [body(): lax.psum_scatter(input_part, 'role', scatter_dimension=0, tiled=True)]
  transfers between devices with their start and end apart: 8 -> 8, of which waited for: 6 -> 6; matrix products, arithmetic and copies ran while one was open for 9% -> 10% of each run, Pallas kernels for 0% -> 0%
where the time goes in v1:
time: 321 us; the launch traced here: 320 us
  blocking collectives  130 us (40%)
  waiting for transfers between devices  119 us (37%)
  matrix products  47.2 us (15%)
  between operations  14.9 us (5%)
  other arithmetic  5.16 us (2%)
  local copies, waits for them, and re-layouts  4.53 us (1%)
    all_gather x1, blocking collectives, body(): lax.all_gather(output_send, ('role', 'dp'), axis=0, tiled=True)  33.3 us
    all_gather x1, blocking collectives, body(): lax.all_gather(output_factor.astype(jnp.bfloat16), ('role', 'dp'), axis=0...  32.9 us
    psum x1, waiting for transfers between devices, body(): low_input, low_grad = lax.psum((low_input, low_grad), 'tp')  32.8 us
    all_gather x1, blocking collectives, body(): lax.all_gather(input_send, ('role', 'dp'), axis=0, tiled=True)  32.7 us
    all_gather x1, blocking collectives, body(): lax.all_gather(input_factor.astype(jnp.bfloat16), ('role', 'dp'), axis=0,...  30.7 us
    dot_general x3, matrix products, contract_rows(): lax.dot_general(left, right, (((0,), (0,)), ((), ())), preferred_element_...  28.1 us
    reduce_scatter x1, waiting for transfers between devices, body(): lax.psum_scatter(output_part, 'role', scatter_dimension=0, tiled=True)  23.7 us
    reduce_scatter x1, waiting for transfers between devices, body(): lax.psum_scatter(input_part, 'role', scatter_dimension=0, tiled=True)  23.5 us
  transfers between devices with their start and end apart: 8, of which 6 were waited for; matrix products, arithmetic and copies ran while one was open for 10% of the time, Pallas kernels for 0%

profile of v1, /device:TPU:0, one launch (start us, length us, event | category | flops | bytes accessed | tf_op | source)
XLA Modules:
  0.0 320.3 jit_solution(4609804505396447305)
XLA Ops:
  7.2 1.0 convert_element_type.31
  8.3 32.9 %all_gather.24 = bf16[64,3584]{1,0:T(8,128)(2,1)S(1)} all-gather(bf16[8,3584]{1,0:T(8,128)(2,1)S(1)} %convert_element_type.31), channel_id=1, replica_groups=mesh['role'=4,'dp'=2,'tp'=4] {'role','dp'}, dimensions={0}, use_global_device_ids=true | all-gather | bytes 516096 | tf_op jit(solution)/shard_map/all_gather | solution.py:59
  41.1 0.9 convert_element_type.34
  42.1 30.7 %all_gather.25 = bf16[64,2048]{1,0:T(8,128)(2,1)S(1)} all-gather(bf16[8,2048]{1,0:T(8,128)(2,1)S(1)} %convert_element_type.34), channel_id=1, replica_groups=mesh['role'=4,'dp'=2,'tp'=4] {'role','dp'}, dimensions={0}, use_global_device_ids=true | all-gather | bytes 294912 | tf_op jit(solution)/shard_map/all_gather | solution.py:58
  72.8 1.3 fusion.8
  74.1 2.4 fusion.9
  77.2 32.8 %all-reduce.3.cloned.1.call-done = (f32[256,64]{1,0:T(8,128)}, f32[256,64]{1,0:T(8,128)}) async-done(((f32[256,64]{1,0:T(8,128)}, f32[256,64]{1,0:T(8,128)}), (f32[256,64]{1,0:T(8,128)}, f32[256,64]{1,0:T(8,128)})) %all-reduce.3.cloned.1.call-update) | async-done | bytes 131088 | tf_op jit(solution)/shard_map/psum | solution.py:63
  110.0 2.3 fusion.2
  112.3 0.0 reduce-scatter.5.cloned.1.call-start
  112.4 2.0 fusion.1
  114.5 23.7 %reduce-scatter.9.cloned.1.call-done = f32[16,3584]{1,0:T(8,128)} async-done(((f32[64,3584]{1,0:T(8,128)}), f32[16,3584]{1,0:T(8,128)}) %reduce-scatter.9.cloned.1.call-update) | async-done | bytes 229392 | tf_op jit(solution)/shard_map/reduce_scatter | solution.py:70
  138.2 23.5 %reduce-scatter.5.cloned.1.call-done = f32[16,2048]{1,0:T(8,128)} async-done(((f32[64,2048]{1,0:T(8,128)}), f32[16,2048]{1,0:T(8,128)}) %reduce-scatter.5.cloned.1.call-update) | async-done | bytes 131088 | tf_op jit(solution)/shard_map/reduce_scatter | solution.py:69
  161.8 11.7 %reduce-scatter.11.cloned.1.call-done = f32[8,3584]{1,0:T(8,128)} async-done(((f32[16,3584]{1,0:T(8,128)}), f32[8,3584]{1,0:T(8,128)}) %reduce-scatter.11.cloned.1.call-update) | async-done | bytes 114704 | tf_op jit(solution)/shard_map/reduce_scatter | solution.py:74
  173.5 1.7 fusion.6
  175.2 33.3 %all_gather.26 = bf16[64,3584]{1,0:T(8,128)(2,1)} all-gather(bf16[8,3584]{1,0:T(8,128)(2,1)S(1)} %get-tuple-element.10), channel_id=1, replica_groups=mesh['role'=4,'dp'=2,'tp'=4] {'role','dp'}, dimensions={0}, use_global_device_ids=true | all-gather | bytes 516096 | tf_op jit(solution)/shard_map/all_gather | solution.py:87
  208.6 1.5 fusion.7
  210.1 32.7 %all_gather.29 = bf16[64,2048]{1,0:T(8,128)(2,1)} all-gather(bf16[8,2048]{1,0:T(8,128)(2,1)S(1)} %get-tuple-element.14), channel_id=1, replica_groups=mesh['role'=4,'dp'=2,'tp'=4] {'role','dp'}, dimensions={0}, use_global_device_ids=true | all-gather | bytes 294912 | tf_op jit(solution)/shard_map/all_gather | solution.py:86
  242.9 0.7 all-gather.7.cloned.1.call-update
  243.7 2.9 copy.19
  246.6 1.6 copy.20
  248.1 11.4 %all-gather.5.cloned.1.call-done = bf16[64,8192]{1,0:T(8,128)(2,1)} async-done(((bf16[64,2048]{1,0:T(8,128)(2,1)}), bf16[64,8192]{1,0:T(8,128)(2,1)}) %all-gather.5.cloned.1.call-update) | async-done | bytes 1048592 | tf_op jit(solution)/shard_map/all_gather | solution.py:90
  259.6 23.8 %add_convert_fusion = bf16[1792,8192]{1,0:T(8,128)(2,1)} fusion(bf16[1792,8192]{1,0:T(8,128)(2,1)} %param.20, bf16[64,8192]{1,0:T(8,128)(2,1)} %all-gather.5.cloned.1.call-done, bf16[64,14336]{1,0:T(8,128)(2,1)} %bitcast.15, s32[]{:T(128)S(6)} %select_n.3), kind=kOutput, calls=%fused_computation | convolution fusion | flops 1937768448 | bytes 59998212 | tf_op jit(solution)/shard_map/dot_general | solution.py:33
  283.3 14.7 %all-gather.7.cloned.1.call-done = bf16[256,8192]{1,0:T(8,128)(2,1)} async-done(((bf16[32,8192]{1,0:T(8,128)(2,1)}), bf16[256,8192]{1,0:T(8,128)(2,1)}) %all-gather.7.cloned.1.call-update) | async-done | bytes 4194320 | tf_op jit(solution)/shard_map/all_gather | solution.py:100
  298.1 15.4 %convolution_convert_fusion = bf16[1792,256]{1,0:T(8,128)(2,1)} fusion(bf16[1792,8192]{1,0:T(8,128)(2,1)} %add_convert_fusion, bf16[256,8192]{1,0:T(8,128)(2,1)} %all-gather.7.cloned.1.call-done), kind=kOutput, calls=%fused_computation.1 | convolution fusion | flops 7516651520 | bytes 34471936 | tf_op jit(solution)/shard_map/dot_general | solution.py:39
  (34 shorter events, 0.5 us)
Async XLA Ops:
  7.2 65.6 %copy-start = (bf16[256,3584]{1,0:T(8,128)(2,1)S(1)}, bf16[256,3584]{1,0:T(8,128)(2,1)}, u32[]{:S(2)}) copy-start(bf16[256,3584]{1,0:T(8,128)(2,1)} %param.12) | copy-start | bytes 5505028
  7.2 102.9 %all-reduce.3.cloned.1.call-start = ((), (), s32[]{:S(2)}) async-start(), calls=%async_computation.11 | async-start | bytes 524288 | tf_op jit(solution)/shard_map/psum | solution.py:63
  41.1 71.3 %copy-start.2 = (bf16[256,2048]{1,0:T(8,128)(2,1)S(1)}, bf16[256,2048]{1,0:T(8,128)(2,1)}, u32[]{:S(2)}) copy-start(bf16[256,2048]{1,0:T(8,128)(2,1)} %param.11) | copy-start | bytes 3145732
  74.1 99.4 %copy-start.3 = (f32[8,3584]{1,0:T(8,128)S(1)}, f32[8,3584]{1,0:T(8,128)}, u32[]{:S(2)}) copy-start(f32[8,3584]{1,0:T(8,128)} %param.17) | copy-start | bytes 344068
  74.1 99.4 %copy-start.5 = (f32[8,3584]{1,0:T(8,128)S(1)}, f32[8,3584]{1,0:T(8,128)}, u32[]{:S(2)}) copy-start(f32[8,3584]{1,0:T(8,128)} %param.18) | copy-start | bytes 344068
  74.1 99.4 %copy-start.6 = (f32[8,3584]{1,0:T(8,128)S(1)}, f32[8,3584]{1,0:T(8,128)}, u32[]{:S(2)}) copy-start(f32[8,3584]{1,0:T(8,128)} %param.19) | copy-start | bytes 344068
  76.4 132.1 %copy-start.4 = (f32[8,2048]{1,0:T(8,128)S(1)}, f32[8,2048]{1,0:T(8,128)}, u32[]{:S(2)}) copy-start(f32[8,2048]{1,0:T(8,128)} %param.14) | copy-start | bytes 196612
  76.4 132.1 %copy-start.7 = (f32[8,2048]{1,0:T(8,128)S(1)}, f32[8,2048]{1,0:T(8,128)}, u32[]{:S(2)}) copy-start(f32[8,2048]{1,0:T(8,128)} %param.15) | copy-start | bytes 196612
  76.4 132.1 %copy-start.8 = (f32[8,2048]{1,0:T(8,128)S(1)}, f32[8,2048]{1,0:T(8,128)}, u32[]{:S(2)}) copy-start(f32[8,2048]{1,0:T(8,128)} %param.16) | copy-start | bytes 196612
  76.5 61.7 %reduce-scatter.9.cloned.1.call-start = ((), (), s32[]{:S(2)}) async-start(), calls=%async_computation.6 | async-start | bytes 1146880 | tf_op jit(solution)/shard_map/reduce_scatter | solution.py:70
  112.3 49.4 %reduce-scatter.5.cloned.1.call-start = ((), (), s32[]{:S(2)}) async-start(), calls=%async_computation.4 | async-start | bytes 655360 | tf_op jit(solution)/shard_map/reduce_scatter | solution.py:69
  114.5 59.1 %reduce-scatter.11.cloned.1.call-start = ((), (), s32[]{:S(2)}) async-start(), calls=%async_computation.7 | async-start | bytes 344064 | tf_op jit(solution)/shard_map/reduce_scatter | solution.py:74
  138.2 70.3 %reduce-scatter.7.cloned.1.call-start = ((), (), s32[]{:S(2)}) async-start(), calls=%async_computation.5 | async-start | bytes 196608 | tf_op jit(solution)/shard_map/reduce_scatter | solution.py:73
  161.8 81.9 %all-gather.9.cloned.1.call-start = ((), (), s32[]{:S(2)}) async-start(), calls=%async_computation.10 | async-start | bytes 2293760 | tf_op jit(solution)/shard_map/all_gather | solution.py:91
  208.5 51.1 %all-gather.5.cloned.1.call-start = ((), (), s32[]{:S(2)}) async-start(), calls=%async_computation.8 | async-start | bytes 1310720 | tf_op jit(solution)/shard_map/all_gather | solution.py:90
  242.9 55.2 %all-gather.7.cloned.1.call-start = ((), (), s32[]{:S(2)}) async-start(), calls=%async_computation.9 | async-start | bytes 4718592 | tf_op jit(solution)/shard_map/all_gather | solution.py:100
  298.1 15.4 %copy-start.1 = (bf16[256,3584]{1,0:T(8,128)(2,1)S(1)}, bf16[256,3584]{1,0:T(8,128)(2,1)}, u32[]{:S(2)}) copy-start(bf16[256,3584]{1,0:T(8,128)(2,1)} %param.12) | copy-start | bytes 5505028
Sparse Core Ops, SparseCore 0:
  76.6 33.4 all-reduce.2
  112.9 25.2 reduce-scatter.8
  141.0 20.6 reduce-scatter.4
  163.8 9.6 reduce-scatter.10
  175.6 10.9 reduce-scatter.6
  208.6 20.8 all-gather.8
  243.0 16.5 all-gather.4
  261.4 36.5 all-gather.6
